TPU v7x, 32 devices: a whole 2x2x4 slice. The times are simulated.
32 devices in a mesh: groups: 2 (over x), seq: 8 (over z, y), dec: 2 (over core).
Axes of the slice: x: 2, y: 2, z: 4, core: 2. Of those that a mesh axis runs over, the one named last changes fastest.
Arguments:
- tokens: bfloat16 [2048, 4096], P(('groups', 'seq')), parts along dimension 0, may hold values from -64 to 64
- norm_gain: float32 [4096], replicated, may hold values from 0.25 to 1.75
- w_query: bfloat16 [4096, 2048], P('seq', 'dec'), may hold values from -0.140625 to 0.140625
- w_key: bfloat16 [4096, 512], P('seq', 'dec'), may hold values from -0.140625 to 0.140625
- w_value: bfloat16 [4096, 512], P('seq', 'dec'), may hold values from -0.09375 to 0.09375
- block_order: int32 [32], P('groups'), parts along dimension 0, may hold values from 0 to 15, as said below
- block_docs: int32 [32], P('groups'), parts along dimension 0, may hold values from 0 to 3, never falling along the last dimension, each value on 1 to 8 neighbouring positions
- head_owner: int32 [8], P('groups'), parts along dimension 0, may hold values from 0 to 3, as said below
- prev_kv: bfloat16 [2048, 2, 4, 128], P(('groups', 'seq', 'dec')), parts along dimension 0, may hold values from -6 to 6
Outputs:
- attended: bfloat16 [2048, 2048], P(('groups', 'seq'), 'dec'), parts along dimension 0
- decode_cache: bfloat16 [2048, 2, 4, 128], P(('groups', 'seq'), None, 'dec'), parts along dimension 0
There are 2 independent parts, one for each index of `groups`. A program takes and returns all parts, laid end to end along the dimension named above; an argument that names none is the same for every part. Nothing has to cross between parts.
Inputs may be any that keep to these rules, and one draw needn't show every extreme that they name: `block_order`: cycle slots 2i and 2i + 1 hold the blocks b and 15 - b for some b; every block stands in exactly one slot. `head_owner`: each key-value head stands in exactly one decode slot.
All inputs are finite; a program needn't handle non-finite values.
Results may differ from a plain program's by a relative error of at most 0.0035.
The roundings to bfloat16 on the way count: a program that leaves them out, or rounds other values in their place, can miss the bound.
Values may be sent and summed in bfloat16 or wider, within the bound.
A program may use at most 64 MiB of HBM per device.

v0:
```python
import math

import jax
import jax.numpy as jnp
from jax import lax
from jax.sharding import PartitionSpec as P

HD = 128


def rotate(values, positions):
    half_width = values.shape[-1] // 2
    frequency = 500000.0 ** (-jnp.arange(half_width, dtype=jnp.float32) / half_width)
    angles = positions[:, None].astype(jnp.float32) * frequency[None, :]
    cosines = jnp.cos(angles)[:, None, :]
    sine_terms = jnp.sin(angles)[:, None, :]
    lower_half = values[..., :half_width]
    upper_half = values[..., half_width:]
    return jnp.concatenate(
        [
            lower_half * cosines - upper_half * sine_terms,
            upper_half * cosines + lower_half * sine_terms,
        ],
        -1,
    )


def per_device(
    tokens, norm_gain, w_query, w_key, w_value, block_order, block_docs, head_owner, prev_kv
):
    rows_dev = tokens.shape[0]
    block_rows = rows_dev // 2
    inputs = tokens.astype(jnp.float32)
    normed = (
        inputs * lax.rsqrt(jnp.mean(inputs * inputs, -1, keepdims=True) + 1e-05) * norm_gain
    ).astype(jnp.bfloat16)

    def add_piece(piece):
        return jnp.dot(normed, piece, preferred_element_type=jnp.float32)

    pieces = (
        lax.all_gather(w_query, "seq", axis=0, tiled=True),
        lax.all_gather(w_key, "seq", axis=0, tiled=True),
        lax.all_gather(w_value, "seq", axis=0, tiled=True),
    )
    query_full, key_full, value_full = tuple((add_piece(piece) for piece in pieces))
    total_rows = rows_dev * lax.axis_size("seq")
    row_ids = jnp.arange(total_rows, dtype=jnp.int32)
    natural = jnp.take(block_order, row_ids // block_rows)
    pos_all = natural * block_rows + row_ids % block_rows
    doc_all = jnp.take(block_docs, natural)
    offset = lax.axis_index("seq") * rows_dev
    my_pos = lax.dynamic_slice_in_dim(pos_all, offset, rows_dev)
    my_doc = lax.dynamic_slice_in_dim(doc_all, offset, rows_dev)
    local_kv = key_full.shape[1] // HD
    local_heads = query_full.shape[1] // HD
    group_size = local_heads // local_kv
    queries = rotate(query_full.reshape(rows_dev, local_heads, HD), my_pos).astype(jnp.bfloat16)
    query_groups = queries.reshape(rows_dev, local_kv, group_size, HD).transpose(1, 2, 0, 3)
    key_rows = (
        rotate(key_full.reshape(rows_dev, local_kv, HD), my_pos)
        .astype(jnp.bfloat16)
        .reshape(rows_dev, local_kv * HD)
    )
    value_rows = value_full.astype(jnp.bfloat16)
    scale = 1.0 / math.sqrt(HD)
    start_max = jnp.full((local_kv, group_size, rows_dev, 1), -jnp.inf, jnp.float32)
    start_sum = jnp.zeros((local_kv, group_size, rows_dev, 1), jnp.float32)
    start_weighted = jnp.zeros((local_kv, group_size, rows_dev, HD), jnp.float32)
    key_piece = lax.all_gather(key_rows, "seq", axis=0, tiled=True)
    value_piece = lax.all_gather(value_rows, "seq", axis=0, tiled=True)
    count = key_piece.shape[0]
    allowed = (pos_all[None, :] <= my_pos[:, None]) & (doc_all[None, :] == my_doc[:, None])

    def update(state):
        running_max, running_sum, weighted = state
        scores = (
            jnp.einsum(
                "ghtd,sgd->ghts",
                query_groups,
                key_piece.reshape(count, local_kv, HD),
                preferred_element_type=jnp.float32,
            )
            * scale
        )
        scores = jnp.where(allowed, scores, -jnp.inf)
        new_max = jnp.max(scores, -1, keepdims=True)
        shift_by = jnp.where(new_max == -jnp.inf, 0.0, new_max)
        weights = jnp.exp(scores - shift_by)
        rescale = jnp.exp(running_max - shift_by)
        running_sum = running_sum * rescale + jnp.sum(weights, -1, keepdims=True)
        weighted = weighted * rescale + jnp.einsum(
            "ghts,sgd->ghtd",
            weights.astype(jnp.bfloat16),
            value_piece.reshape(count, local_kv, HD),
            preferred_element_type=jnp.float32,
        )
        return (new_max, running_sum, weighted)

    final_max, final_sum, final_weighted = lax.cond(
        jnp.any(allowed), update, lambda state: state, (start_max, start_sum, start_weighted)
    )
    attended = (
        (final_weighted / final_sum)
        .transpose(2, 0, 1, 3)
        .reshape(rows_dev, local_heads * HD)
        .astype(jnp.bfloat16)
    )
    head_count = prev_kv.shape[2]
    selector = (head_owner[:, None] == jnp.arange(head_count, dtype=jnp.int32)[None, :]).astype(
        jnp.bfloat16
    )
    ordered = jnp.einsum(
        "tcjd,sj->tcsd", prev_kv, selector, preferred_element_type=jnp.float32
    ).astype(jnp.bfloat16)
    decode_cache = lax.all_to_all(ordered, "dec", split_axis=2, concat_axis=0, tiled=True)
    return (attended, decode_cache)


def solution(mesh):
    in_specs = (
        P(("groups", "seq"), None),
        P(),
        P("seq", "dec"),
        P("seq", "dec"),
        P("seq", "dec"),
        P("groups"),
        P("groups"),
        P("groups"),
        P(("groups", "seq", "dec"), None, None, None),
    )
    out_specs = (P(("groups", "seq"), "dec"), P(("groups", "seq"), None, "dec", None))
    return jax.shard_map(
        per_device, mesh=mesh, in_specs=in_specs, out_specs=out_specs, check_vma=False
    )
```

profile of v0, /device:TPU:0, one launch (start us, length us, event | category | flops | bytes accessed | tf_op | source)
XLA Modules:
  0.0 262.9 jit_solution(15112407311073166945)
XLA Ops:
  7.2 0.0 copy-start
  7.2 0.0 all-gather.4.cloned.1.call-start
  7.2 0.7 all-gather.4.cloned.1.call-update
  7.9 0.0 all-gather.8.cloned.1.call-start
  8.0 0.7 all-gather.8.cloned.1.call-update
  8.7 0.0 all-gather.6.cloned.1.call-start
  8.7 0.7 all-gather.6.cloned.1.call-update
  9.4 0.0 copy-done
  9.4 0.0 copy-start.2
  9.4 0.0 copy-start.3
  9.4 1.0 fusion.21
  10.4 0.8 copy.22
  11.2 3.4 %all-to-all-start = ((bf16[64,2,4,128]{3,1,0,2:T(2,128)(2,1)}), bf16[64,2,4,128]{3,1,0,2:T(2,128)(2,1)S(1)}, u32[]{:S(2)}, u32[]{:S(2)}) async-start(bf16[64,2,4,128]{3,1,0,2:T(2,128)(2,1)} %copy.22), calls=%async_computation | async-start | bytes 262144 | tf_op jit(solution)/shard_map/all_to_all | solution.py:116
  14.6 2.0 fusion.58
  16.6 1.9 fusion.59
  18.5 19.9 %select_select_fusion = s32[1024]{0:T(1024)S(1)} fusion(s32[]{:T(128)} %bitcast.35, s32[]{:T(128)} %bitcast.34, s32[]{:T(128)} %bitcast.33, s32[]{:T(128)} %bitcast.32, s32[]{:T(128)} %bitcast.31, s32[]{:T(128)} %bitcast.30, s32[]{:T(128)} %bitcast.29, s32[]{:T(128)} %bitcast.28, s32[]{:T(128)} %bitcast.27, s32[]{:T(128)} %bitcast.26, s32[]{:T(128)} %bitcast.25, ...), kind=kLoop, calls=%fused_computation.72 | loop fusion | flops 83968 | bytes 4224 | tf_op jit(solution)/shard_map/jit(_take)/select_n | solution.py:51
  38.4 0.1 dynamic_slice.7
  38.5 10.0 %fusion.29 = s32[1024]{0:T(1024)S(1)} fusion(s32[]{:T(128)} %bitcast.19, s32[]{:T(128)} %bitcast.18, s32[]{:T(128)} %bitcast.17, s32[]{:T(128)} %bitcast.16, s32[]{:T(128)} %bitcast.15, s32[]{:T(128)} %bitcast.14, s32[]{:T(128)} %bitcast.13, s32[]{:T(128)} %bitcast.12, s32[]{:T(128)} %bitcast.11, s32[]{:T(128)} %bitcast.10, s32[]{:T(128)} %bitcast.9, ...), kind=kLoop, calls=%fused_computation.53 | loop fusion | flops 52224 | bytes 4160 | tf_op jit(solution)/shard_map/add | solution.py:50
  48.5 0.1 fusion.56
  48.6 0.8 fusion.57
  50.0 0.0 all-to-all-done
  50.1 0.9 copy.23
  50.9 1.5 fusion.18
  52.5 0.3 multiply_cosine_fusion
  52.8 9.2 %all-gather.4.cloned.1.call-done = bf16[4096,256]{1,0:T(8,128)(2,1)} async-done(((bf16[512,256]{1,0:T(8,128)(2,1)}), bf16[4096,256]{1,0:T(8,128)(2,1)}) %all-gather.4.cloned.1.call-update) | async-done | bytes 2097168 | tf_op jit(solution)/shard_map/all_gather | solution.py:43
  62.0 2.4 fusion.54
  64.5 0.1 reshape.133
  64.5 0.3 subtract_convert_fusion.1
  64.8 0.2 pad_maximum_fusion
  65.0 32.8 %all_gather.16 = bf16[1024,256]{1,0:T(8,128)(2,1)S(1)} all-gather(bf16[128,256]{1,0:T(8,128)(2,1)S(1)} %bitcast.75), channel_id=1, replica_groups=mesh['groups'=2,'seq'=8,'dec'=2] {'seq'}, dimensions={0}, use_global_device_ids=true | all-gather | bytes 589824 | tf_op jit(solution)/shard_map/all_gather | solution.py:70
  97.8 15.3 %all-gather.8.cloned.1.call-done = bf16[4096,256]{1,0:T(8,128)(2,1)} async-done(((bf16[512,256]{1,0:T(8,128)(2,1)}), bf16[4096,256]{1,0:T(8,128)(2,1)}) %all-gather.8.cloned.1.call-update) | async-done | bytes 2097168 | tf_op jit(solution)/shard_map/all_gather | solution.py:44
  113.1 0.0 copy-done.2
  113.1 0.0 copy-done.3
  113.1 2.1 convolution_convert_fusion.1
  115.2 33.3 %all_gather.19 = bf16[1024,256]{1,0:T(8,128)(2,1)S(1)} all-gather(bf16[128,256]{1,0:T(8,128)(2,1)S(1)} %convolution_convert_fusion.1), channel_id=1, replica_groups=mesh['groups'=2,'seq'=8,'dec'=2] {'seq'}, dimensions={0}, use_global_device_ids=true | all-gather | bytes 589824 | tf_op jit(solution)/shard_map/all_gather | solution.py:71
  148.5 93.5 %all-gather.6.cloned.1.call-done = bf16[4096,1024]{1,0:T(8,128)(2,1)} async-done(((bf16[512,1024]{1,0:T(8,128)(2,1)}), bf16[4096,1024]{1,0:T(8,128)(2,1)}) %all-gather.6.cloned.1.call-update) | async-done | bytes 8388624 | tf_op jit(solution)/shard_map/all_gather | solution.py:42
  242.0 4.7 %convolution_bitcast_fusion = f32[16,8,8,128]{3,1,2,0:T(8,128)S(1)} fusion(bf16[4096,1024]{1,0:T(8,128)(2,1)} %all-gather.6.cloned.1.call-done, bf16[128,4096]{1,0:T(8,128)(2,1)S(1)} %copy-done.2, f32[4096]{0:T(1024)S(1)} %copy-done.3, f32[128]{0:T(128)S(1)} %add_rsqrt_fusion), kind=kOutput, calls=%fused_computation.25 | convolution fusion | flops 1075838976 | bytes 9978368 | tf_op jit(solution)/shard_map/dot_general | solution.py:39
  246.7 0.1 copy.32
  246.8 0.3 subtract_convert_fusion
  247.1 0.1 maximum_bitcast_fusion
  247.3 7.8 %conditional.1 = (f32[2,4,128,1]{2,1,0,3:T(4,128)S(1)}, f32[2,4,128,128]{3,2,1,0:T(8,128)S(1)}) conditional(s32[]{:T(128)} %convert_element_type.43, () %tuple.17, (pred[128,1024]{1,0:T(8,128)(4,1)S(1)}, bf16[1024,256]{1,0:T(8,128)(2,1)S(1)}, bf16[2,4,128,128]{3,2,1,0:T(8,128)(2,1)S(1)}, bf16[1024,256]{1,0:T(8,128)(2,1)S(1)}) %tuple.18), branch_computations={%region_2.4_spmd, %region_3.7_spmd} | conditional | flops 548543488 | bytes 33730604 | solution.py:100
  247.3 0.1 reshape.129
  247.4 2.8 %fusion = (f32[2,4,128]{2,1,0:T(4,128)S(1)}, f32[2,4,128,1024]{3,2,1,0:T(8,128)}) fusion(pred[128,1024]{1,0:T(8,128)(4,1)S(1)} %get-tuple-element.3, bf16[2,4,128,128]{3,2,1,0:T(8,128)(2,1)S(1)} %get-tuple-element.10, bf16[1024,2,128,1]{2,1,0,3:T(2,128)(2,1)S(1)} %bitcast.69), kind=kOutput, calls=%fused_computation.2 | convolution fusion | flops 271580160 | bytes 5115904 | tf_op jit(solution)/shard_map/cond/branch_1_fun/ghtd,sgd->ghts/dot_general | solution.py:78
  250.2 0.1 reshape.130
  250.4 0.0 copy-start.1
  250.4 3.5 %fusion.6 = f32[2,4,128,128]{3,2,1,0:T(8,128)S(1)} fusion(f32[2,4,128,1024]{3,2,1,0:T(8,128)} %get-tuple-element.26, f32[2,4,128]{2,1,0:T(4,128)S(1)} %get-tuple-element.24, pred[128,1024]{1,0:T(8,128)(4,1)S(1)} %get-tuple-element.3, bf16[1024,2,128,1]{2,1,0,3:T(2,128)(2,1)S(1)} %bitcast.72, f32[2,4,128]{2,1,0:T(4,128)S(1)} %get-tuple-element.23), kind=kOutput, calls=%fused_computation.7 | convolution fusion | flops 272760832 | bytes 5382144 | tf_op jit(solution)/shard_map/cond/branch_1_fun/ghts,sgd->ghtd/dot_general | solution.py:92
  253.9 0.0 copy-done.1
  253.9 1.1 fusion.2
  255.1 0.2 fusion.22
  255.3 0.2 copy.21
  255.5 0.9 convert_element_type.51
  (7 shorter events, 0.1 us)
Async XLA Ops:
  7.2 2.2 copy-start
  7.2 54.9 %all-gather.4.cloned.1.call-start = ((), (), s32[]{:S(2)}) async-start(), calls=%async_computation.1 | async-start | bytes 2359296 | tf_op jit(solution)/shard_map/all_gather | solution.py:43
  7.9 105.2 %all-gather.8.cloned.1.call-start = ((), (), s32[]{:S(2)}) async-start(), calls=%async_computation.3 | async-start | bytes 2359296 | tf_op jit(solution)/shard_map/all_gather | solution.py:44
  8.7 233.3 %all-gather.6.cloned.1.call-start = ((), (), s32[]{:S(2)}) async-start(), calls=%async_computation.2 | async-start | bytes 9437184 | tf_op jit(solution)/shard_map/all_gather | solution.py:42
  9.4 103.7 %copy-start.2 = (bf16[128,4096]{1,0:T(8,128)(2,1)S(1)}, bf16[128,4096]{1,0:T(8,128)(2,1)}, u32[]{:S(2)}) copy-start(bf16[128,4096]{1,0:T(8,128)(2,1)} %param.13) | copy-start | bytes 3145732
  9.4 103.7 %copy-start.3 = (f32[4096]{0:T(1024)S(1)}, f32[4096]{0:T(1024)}, u32[]{:S(2)}) copy-start(f32[4096]{0:T(1024)} %param.14) | copy-start | bytes 49156
  11.2 38.8 %all-to-all-start = ((bf16[64,2,4,128]{3,1,0,2:T(2,128)(2,1)}), bf16[64,2,4,128]{3,1,0,2:T(2,128)(2,1)S(1)}, u32[]{:S(2)}, u32[]{:S(2)}) async-start(bf16[64,2,4,128]{3,1,0,2:T(2,128)(2,1)} %copy.22), calls=%async_computation | async-start | bytes 262144 | tf_op jit(solution)/shard_map/all_to_all | solution.py:116
  250.4 3.6 %copy-start.1 = (f32[2,4,128,1024]{3,2,1,0:T(8,128)S(1)}, f32[2,4,128,1024]{3,2,1,0:T(8,128)}, u32[]{:S(2)}) copy-start(f32[2,4,128,1024]{3,2,1,0:T(8,128)} %get-tuple-element.26) | copy-start | bytes 12582916 | tf_op jit(solution)/shard_map/cond
Sparse Core Ops, SparseCore 0:
  10.1 51.8 all-gather.3
  64.2 48.8 all-gather.7
  115.2 126.7 all-gather.5
where the time goes:
time: 264 us; the launch traced here: 263 us
  waiting for transfers between devices  120 us (45%)
  blocking collectives  66.1 us (25%)
  other arithmetic  34.9 us (13%)
  matrix products  16.5 us (6%)
  between operations  14.6 us (6%)
  local copies, waits for them, and re-layouts  7.21 us (3%)
  starting transfers between devices  3.49 us (1%)
    all_gather x1, waiting for transfers between devices, per_device(): lax.all_gather(w_query, 'seq', axis=0, tiled=True)  93.5 us
    all_gather x1, blocking collectives, per_device(): value_piece = lax.all_gather(value_rows, 'seq', axis=0, tiled=True)  33.3 us
    all_gather x1, blocking collectives, per_device(): key_piece = lax.all_gather(key_rows, 'seq', axis=0, tiled=True)  32.8 us
    select_n x1, other arithmetic, per_device(): doc_all = jnp.take(block_docs, natural)  19.9 us
    all_gather x1, waiting for transfers between devices, per_device(): lax.all_gather(w_value, 'seq', axis=0, tiled=True)  15.3 us
    add x1, other arithmetic, per_device(): pos_all = natural * block_rows + row_ids % block_rows  9.98 us
    all_gather x1, waiting for transfers between devices, per_device(): lax.all_gather(w_key, 'seq', axis=0, tiled=True)  9.24 us
    dot_general x3, matrix products, add_piece(): return jnp.dot(normed, piece, preferred_element_type=jnp.float32)  9.16 us
  transfers between devices with their start and end apart: 4, of which 3 were waited for; matrix products, arithmetic and copies ran while one was open for 17% of the time, Pallas kernels for 0%

commit v1 on v0

--- a/solution.py
+++ b/solution.py
@@ -1,8 +1,11 @@
+import functools
 import math
 
 import jax
 import jax.numpy as jnp
 from jax import lax
+from jax.experimental import pallas as pl
+from jax.experimental.pallas import tpu as pltpu
 from jax.sharding import PartitionSpec as P
 
 HD = 128
@@ -25,7 +28,7 @@
     )
 
 
-def per_device(
+def general_plan(
     tokens, norm_gain, w_query, w_key, w_value, block_order, block_docs, head_owner, prev_kv
 ):
     rows_dev = tokens.shape[0]
@@ -117,6 +120,525 @@
     return (attended, decode_cache)
 
 
+def attend_kernel(
+    sizes,
+    order_ref,
+    docs_ref,
+    freq_ref,
+    gain_ref,
+    tok_in,
+    wq_in,
+    wk_in,
+    wv_in,
+    prev_in,
+    out_ref,
+    prev_out,
+    tok,
+    wbuf,
+    normed,
+    qbuf,
+    kvbuf,
+    csbuf,
+    att,
+    local_sem,
+    home_send,
+    homeq_recv,
+    homekv_recv,
+    rel_send,
+    rel_recv,
+    own_send,
+    fwd_send,
+    tok_recv,
+    sib_send,
+    sib_recv,
+    prev_sem,
+    kv_send,
+    kv_recv,
+    att_send,
+    att_recv,
+):
+    X, A, Y, rows, R, hpg, slots, blk, T = sizes
+    Rp = R // X
+    half = rows // 2
+    QW = hpg * HD
+    x = lax.axis_index("groups")
+    q = lax.axis_index("seq")
+    d = lax.axis_index("dec")
+    a = q // Y
+    y = q % Y
+    unit = a % 2
+
+    def dev(x_, a_, y_, d_=None):
+        return {"groups": x_, "seq": a_ * Y + y_, "dec": d if d_ is None else d_}
+
+    def remote(src, dst, ssem, rsem, device):
+        return pltpu.make_async_remote_copy(
+            src_ref=src,
+            dst_ref=dst,
+            send_sem=ssem,
+            recv_sem=rsem,
+            device_id=device,
+            device_id_type=pl.DeviceIdType.MESH,
+        )
+
+    sibling = dev(x, a, y, 1 - d)
+    barrier = pltpu.get_barrier_semaphore()
+    plane = [(i, j) for i in range(X) for j in range(Y) if (i, j) != (0, 0)]
+    peers = [dev((x + i) % X, a, (y + j) % Y) for i, j in plane]
+    peers += [dev(x, (a + t) % A, y) for t in range(1, A)]
+    mate = a + 1 - 2 * unit
+    peers += [dev(x, mate, (y + j) % Y) for j in range(1, Y)]
+    peers.append(sibling)
+    for peer in peers:
+        pl.semaphore_signal(barrier, inc=1, device_id=peer, device_id_type=pl.DeviceIdType.MESH)
+    pl.semaphore_wait(barrier, len(peers))
+
+    def w_rows(a_, y_, x_):
+        return pl.ds(pl.multiple_of((a_ * Y + y_) * R + x_ * Rp, Rp), Rp)
+
+    part = pl.ds(pl.multiple_of(x * Rp, Rp), Rp)
+
+    def kv_source(t):
+        return wv_in if t % 2 else wk_in
+
+    def home_copies(t):
+        kv_cols = pl.ds((t // 2) * HD, HD)
+        return (
+            remote(
+                wq_in.at[part, pl.ds(t * QW, QW)],
+                wbuf.at[w_rows(a, y, x), pl.ds(0, QW)],
+                home_send.at[0, t],
+                homeq_recv.at[a],
+                dev(x, t, y),
+            ),
+            remote(
+                kv_source(t).at[part, kv_cols],
+                wbuf.at[w_rows(a, y, x), pl.ds(QW, HD)],
+                home_send.at[1, t],
+                homekv_recv.at[a],
+                dev(x, t, y),
+            ),
+        )
+
+    def local_copies(t):
+        rows_all = pl.ds(pl.multiple_of(q * R, R), R)
+        return (
+            pltpu.make_async_copy(
+                wq_in.at[:, pl.ds(t * QW, QW)],
+                wbuf.at[rows_all, pl.ds(0, QW)],
+                local_sem.at[0],
+            ),
+            pltpu.make_async_copy(
+                kv_source(t).at[:, pl.ds((t // 2) * HD, HD)],
+                wbuf.at[rows_all, pl.ds(QW, HD)],
+                local_sem.at[1],
+            ),
+        )
+
+    for t in range(A):
+
+        @pl.when(a == t)
+        def _():
+            for copy in local_copies(t):
+                copy.start()
+
+        @pl.when(a != t)
+        def _():
+            for copy in home_copies(t):
+                copy.start()
+
+    my_half = pl.ds(pl.multiple_of(d * half, half), half)
+    other_half = pl.ds(pl.multiple_of((1 - d) * half, half), half)
+
+    def own_push(side):
+        return remote(
+            tok_in.at[my_half],
+            tok.at[a, my_half],
+            own_send.at[side],
+            tok_recv.at[a],
+            dev(x, a + 1 - 2 * side, y),
+        )
+
+    @pl.when(a + 1 < A)
+    def _():
+        own_push(0).start()
+
+    @pl.when(a >= 1)
+    def _():
+        own_push(1).start()
+
+    own_tok = pltpu.make_async_copy(tok_in, tok.at[a], local_sem.at[2])
+    own_tok.start()
+    prev_copy = remote(prev_in, prev_out, prev_sem.at[0], prev_sem.at[1], sibling)
+    prev_copy.start()
+
+    def relay(t, index, i, j):
+        src = wbuf.at[w_rows(t, y, x)]
+        return remote(
+            src,
+            src,
+            rel_send.at[t, index],
+            rel_recv.at[t, y, x],
+            dev((x + i) % X, a, (y + j) % Y),
+        )
+
+    for t in range(A):
+
+        @pl.when(a == t)
+        def _():
+            for copy in local_copies(t):
+                copy.wait()
+            for index, (i, j) in enumerate(plane):
+                if j:
+                    relay(t, index, i, j).start()
+
+    lane = lax.broadcasted_iota(jnp.int32, (rows, HD), 1)
+    row_id = lax.broadcasted_iota(jnp.int32, (rows, 1), 0)
+
+    def row_values(c, table):
+        value = jnp.zeros((rows, 1), jnp.int32)
+        for i in range(slots):
+            entry = table(order_ref[(c * Y + y) * slots + i])
+            value = jnp.where(row_id // blk == i, entry, value)
+        return value
+
+    def row_positions(c):
+        return row_values(c, lambda n: n) * blk + row_id % blk
+
+    def angles(c, carry):
+        angle = row_positions(c).astype(jnp.float32) * freq_ref[...]
+        csbuf[0, c] = jnp.cos(angle)
+        sine = jnp.sin(angle)
+        csbuf[1, c] = jnp.where(lane < HD // 2, -sine, sine)
+        return carry
+
+    lax.fori_loop(0, A, angles, 0)
+
+    for o in range(1, A):
+        t = (a + o) % A
+        src = wbuf.at[w_rows(t, y, x)]
+        remote(
+            wq_in.at[part, pl.ds(0, QW)],
+            wbuf.at[w_rows(t, y, x), pl.ds(0, QW)],
+            home_send.at[0, 0],
+            homeq_recv.at[t],
+            sibling,
+        ).wait_recv()
+        remote(
+            wk_in.at[part, pl.ds(0, HD)],
+            wbuf.at[w_rows(t, y, x), pl.ds(QW, HD)],
+            home_send.at[1, 0],
+            homekv_recv.at[t],
+            sibling,
+        ).wait_recv()
+        for index, (i, j) in enumerate(plane):
+            relay(t, index, i, j).start()
+
+    def forward(c, to):
+        return remote(
+            tok.at[c, my_half],
+            tok.at[c, my_half],
+            fwd_send.at[c],
+            tok_recv.at[c],
+            dev(x, to, y),
+        )
+
+    def share(c):
+        return remote(
+            tok.at[c, my_half], tok.at[c, my_half], sib_send.at[c], sib_recv.at[c], sibling
+        )
+
+    for s in range(1, A):
+
+        @pl.when(a >= s)
+        def _():
+            c = a - s
+            forward(c, a).wait_recv()
+
+            @pl.when(a + 1 < A)
+            def _():
+                forward(c, a + 1).start()
+
+            share(c).start()
+
+        @pl.when(a + s < A)
+        def _():
+            c = a + s
+            forward(c, a).wait_recv()
+
+            @pl.when(a >= 1)
+            def _():
+                forward(c, a - 1).start()
+
+            share(c).start()
+
+    own_tok.wait()
+    for o in range(A):
+        t = (a + o) % A
+        for i, j in plane:
+            if o or j:
+                src = wbuf.at[w_rows(t, (y + j) % Y, (x + i) % X)]
+                remote(
+                    src,
+                    src,
+                    rel_send.at[0, 0],
+                    rel_recv.at[t, (y + j) % Y, (x + i) % X],
+                    sibling,
+                ).wait_recv()
+
+    def pick(s):
+        value, bit = 0, 1
+        while bit < A:
+            value = value + bit * ((a // bit + s // bit) % 2)
+            bit *= 2
+        return value
+
+    def kv_peer(dy, da):
+        return dev(x, a - unit + (unit + da) % 2, (y + dy) % Y)
+
+    kv_plan = [(dy, da) for dy in range(Y) for da in range(2) if (dy, da) != (0, 0)]
+
+    def kv_push(s, c, index, dy, da):
+        src = kvbuf.at[unit, c * Y + y]
+        return remote(src, src, kv_send.at[s, index], kv_recv.at[unit, c, y], kv_peer(dy, da))
+
+    def project(s, carry):
+        c = pick(s)
+
+        @pl.when(s > 0)
+        def _():
+            remote(
+                tok.at[c, other_half],
+                tok.at[c, other_half],
+                sib_send.at[c],
+                sib_recv.at[c],
+                sibling,
+            ).wait_recv()
+
+        inputs = tok[c].astype(jnp.float32)
+        mean = jnp.mean(inputs * inputs, -1, keepdims=True)
+        normed[...] = (inputs * lax.rsqrt(mean + 1e-05) * gain_ref[...]).astype(jnp.bfloat16)
+        cosine = csbuf[0, c]
+        sine = csbuf[1, c]
+        product = jnp.dot(normed[...], wbuf[...], preferred_element_type=jnp.float32)
+
+        def turn(v):
+            return v * cosine + pltpu.roll(v, HD // 2, 1) * sine
+
+        raw = product[:, QW:]
+        kvbuf[unit, c * Y + y] = jnp.where(unit == 0, turn(raw), raw).astype(jnp.bfloat16)
+        for h in range(hpg):
+            qbuf[c, :, h * HD : (h + 1) * HD] = turn(product[:, h * HD : (h + 1) * HD]).astype(
+                jnp.bfloat16
+            )
+        for index, (dy, da) in enumerate(kv_plan):
+            kv_push(s, c, index, dy, da).start()
+        return carry
+
+    lax.fori_loop(0, A, project, 0)
+
+    for s in range(A):
+        c = pick(s)
+        for dy, da in kv_plan:
+            u = (unit + da) % 2
+            dst = kvbuf.at[u, c * Y + (y + dy) % Y]
+            remote(
+                dst, dst, kv_send.at[0, 0], kv_recv.at[u, c, (y + dy) % Y], sibling
+            ).wait_recv()
+
+    key_id = lax.broadcasted_iota(jnp.int32, (1, T), 1)
+    key_pos = jnp.zeros((1, T), jnp.int32)
+    key_doc = jnp.zeros((1, T), jnp.int32)
+    for i in range(T // blk):
+        here = key_id // blk == i
+        natural = order_ref[i]
+        key_pos = jnp.where(here, natural * blk, key_pos)
+        key_doc = jnp.where(here, docs_ref[natural], key_doc)
+    key_pos = key_pos + key_id % blk
+    scale = 1.0 / math.sqrt(HD)
+    out_cols = pl.ds(pl.multiple_of(a * QW, QW), QW)
+
+    def att_push(s, c):
+        return remote(
+            att.at[c], out_ref.at[:, out_cols], att_send.at[s], att_recv.at[a], dev(x, c, y)
+        )
+
+    def attend(s, carry):
+        c = pick(A - 1 - s)
+        allowed = (key_pos <= row_positions(c)) & (
+            key_doc == row_values(c, lambda n: docs_ref[n])
+        )
+        keys = kvbuf[0].reshape(T, HD)
+        values = kvbuf[1].reshape(T, HD)
+        for h in range(hpg):
+            scores = (
+                lax.dot_general(
+                    qbuf[c, :, h * HD : (h + 1) * HD],
+                    keys,
+                    (((1,), (1,)), ((), ())),
+                    preferred_element_type=jnp.float32,
+                )
+                * scale
+            )
+            scores = jnp.where(allowed, scores, -jnp.inf)
+            weights = jnp.exp(scores - jnp.max(scores, -1, keepdims=True))
+            total = jnp.sum(weights, -1, keepdims=True)
+            weighted = jnp.dot(
+                weights.astype(jnp.bfloat16), values, preferred_element_type=jnp.float32
+            )
+            att[c, :, h * HD : (h + 1) * HD] = (weighted / total).astype(jnp.bfloat16)
+
+        @pl.when(s < A - 1)
+        def _():
+            att_push(s, c).start()
+
+        return carry
+
+    lax.fori_loop(0, A, attend, 0)
+    own_out = pltpu.make_async_copy(att.at[a], out_ref.at[:, out_cols], local_sem.at[3])
+    own_out.start()
+
+    for t in range(A):
+
+        @pl.when(a != t)
+        def _():
+            for copy in home_copies(t):
+                copy.wait_send()
+            for index, (i, j) in enumerate(plane):
+                relay(t, index, i, j).wait_send()
+
+        @pl.when(a == t)
+        def _():
+            for index, (i, j) in enumerate(plane):
+                if j:
+                    relay(t, index, i, j).wait_send()
+
+    @pl.when(a + 1 < A)
+    def _():
+        own_push(0).wait_send()
+
+    @pl.when(a >= 1)
+    def _():
+        own_push(1).wait_send()
+
+    for s in range(1, A):
+
+        @pl.when(a >= s)
+        def _():
+            share(a - s).wait_send()
+
+            @pl.when(a + 1 < A)
+            def _():
+                forward(a - s, a + 1).wait_send()
+
+        @pl.when(a + s < A)
+        def _():
+            share(a + s).wait_send()
+
+            @pl.when(a >= 1)
+            def _():
+                forward(a + s, a - 1).wait_send()
+
+    for s in range(A):
+        for index, (dy, da) in enumerate(kv_plan):
+            kv_push(s, pick(s), index, dy, da).wait_send()
+    prev_copy.wait()
+    own_out.wait()
+    for s in range(A - 1):
+        att_push(s, pick(A - 1 - s)).wait_send()
+    for o in range(1, A):
+        t = (a + o) % A
+        cols = pl.ds(pl.multiple_of(t * QW, QW), QW)
+        remote(
+            att.at[0], out_ref.at[:, cols], att_send.at[0], att_recv.at[t], sibling
+        ).wait_recv()
+
+
+def column_plan(
+    X, tokens, norm_gain, w_query, w_key, w_value, block_order, block_docs, head_owner, prev_kv
+):
+    n_seq = lax.axis_size("seq")
+    rows, width = tokens.shape
+    R = w_query.shape[0]
+    local_kv = w_key.shape[1] // HD
+    local_heads = w_query.shape[1] // HD
+    A = 2 * local_kv
+    Y = n_seq // A
+    hpg = local_heads // A
+    slots = block_order.shape[0] // n_seq
+    blk = rows // slots
+    T = n_seq * rows
+    QW = hpg * HD
+    frequency = 500000.0 ** (-jnp.arange(HD // 2, dtype=jnp.float32) / (HD // 2))
+    freq = jnp.concatenate([frequency, frequency])[None, :]
+    sizes = (X, A, Y, rows, R, hpg, slots, blk, T)
+    dma = pltpu.SemaphoreType.DMA
+    smem = pl.BlockSpec(memory_space=pltpu.SMEM)
+    vmem = pl.BlockSpec(memory_space=pltpu.VMEM)
+    anywhere = pl.BlockSpec(memory_space=pl.ANY)
+    attended, other = pl.pallas_call(
+        functools.partial(attend_kernel, sizes),
+        out_shape=(
+            jax.ShapeDtypeStruct((rows, local_heads * HD), jnp.bfloat16),
+            jax.ShapeDtypeStruct(prev_kv.shape, prev_kv.dtype),
+        ),
+        in_specs=[smem, smem, vmem, vmem] + [anywhere] * 5,
+        out_specs=(vmem, anywhere),
+        scratch_shapes=[
+            pltpu.VMEM((A, rows, width), jnp.bfloat16),
+            pltpu.VMEM((width, QW + HD), jnp.bfloat16),
+            pltpu.VMEM((rows, width), jnp.bfloat16),
+            pltpu.VMEM((A, rows, QW), jnp.bfloat16),
+            pltpu.VMEM((2, n_seq, rows, HD), jnp.bfloat16),
+            pltpu.VMEM((2, A, rows, HD), jnp.float32),
+            pltpu.VMEM((A, rows, QW), jnp.bfloat16),
+            dma((4,)),
+            dma((2, A)),
+            dma((A,)),
+            dma((A,)),
+            dma((A, X * Y)),
+            dma((A, Y, X)),
+            dma((2,)),
+            dma((A,)),
+            dma((A,)),
+            dma((A,)),
+            dma((A,)),
+            dma((2,)),
+            dma((A, 2 * Y)),
+            dma((2, A, Y)),
+            dma((A,)),
+            dma((A,)),
+        ],
+        compiler_params=pltpu.CompilerParams(
+            collective_id=0, has_side_effects=True, vmem_limit_bytes=48 * 1024 * 1024
+        ),
+    )(
+        block_order,
+        block_docs,
+        freq,
+        norm_gain[None, :],
+        tokens,
+        w_query,
+        w_key,
+        w_value,
+        prev_kv,
+    )
+    d = lax.axis_index("dec")
+    head_count = prev_kv.shape[2]
+    mine = head_count // 2
+    owner = lax.dynamic_slice_in_dim(head_owner, d * mine, mine)
+    both = jnp.concatenate(
+        [jnp.where(d == 0, prev_kv, other), jnp.where(d == 0, other, prev_kv)], 0
+    )
+    picks = []
+    for s in range(mine):
+        chosen = both[:, :, 0]
+        for j in range(1, head_count):
+            chosen = jnp.where(owner[s] == j, both[:, :, j], chosen)
+        picks.append(chosen)
+    return attended, jnp.stack(picks, 2)
+
+
 def solution(mesh):
     in_specs = (
         P(("groups", "seq"), None),
@@ -130,6 +652,23 @@
         P(("groups", "seq", "dec"), None, None, None),
     )
     out_specs = (P(("groups", "seq"), "dec"), P(("groups", "seq"), None, "dec", None))
+    X = mesh.shape["groups"]
+    n_seq = mesh.shape["seq"]
+
+    def per_device(tokens, norm_gain, w_query, w_key, w_value, *rest):
+        A = 2 * (w_key.shape[1] // HD)
+        heads = w_query.shape[1] // HD
+        fits = (
+            mesh.shape["dec"] == 2
+            and A & (A - 1) == 0
+            and n_seq % A == 0
+            and heads % A == 0
+            and w_query.shape[0] % (16 * X) == 0
+            and tokens.shape[0] % 32 == 0
+        )
+        plan = functools.partial(column_plan, X) if fits else general_plan
+        return plan(tokens, norm_gain, w_query, w_key, w_value, *rest)
+
     return jax.shard_map(
         per_device, mesh=mesh, in_specs=in_specs, out_specs=out_specs, check_vma=False
     )

time: 264 us -> 91.4 us (0.35)
  waiting for transfers between devices: 120 us -> 0 us
  Pallas kernels: 0 us -> 76.9 us
  blocking collectives: 66.1 us -> 0 us
  other arithmetic: 34.9 us -> 1.62 us
  matrix products: 16.5 us -> 0 us
  between operations: 14.6 us -> 4.59 us
  starting transfers between devices: 3.49 us -> 0 us
    all_gather x3 -> x0, waiting for transfers between devices: 118 us -> none  [the longest x1 93.5 us: per_device(): lax.all_gather(w_query, 'seq', axis=0, tiled=True)]
    pallas_call x0 -> x1, Pallas kernels: none -> 76.9 us  [column_plan(): pl.pallas_call(functools.partial(attend_kernel, sizes), out_shape=(jax.Sh...]
    all_gather x2 -> x0, blocking collectives: 66.1 us -> none  [the longest x1 33.3 us: per_device(): value_piece = lax.all_gather(value_rows, 'seq', axis=0, tiled=True)]
    select_n x1 -> x2, other arithmetic: 19.9 us -> 0.57 us  [the longest x1 0.55 us: column_plan(): chosen = jnp.where(owner[s] == j, both[:, :, j], chosen)]
    dot_general x6 -> x0, matrix products: 16.5 us -> none  [the longest x3 9.16 us: add_piece(): return jnp.dot(normed, piece, preferred_element_type=jnp.float32)]
    add x2 -> x0, other arithmetic: 10 us -> none  [the longest x1 9.98 us: per_device(): pos_all = natural * block_rows + row_ids % block_rows]
    unnamed x8 -> x19, local copies, waits for them, and re-layouts: 0.13 us -> 7.25 us
    gather x2 -> x0, local copies, waits for them, and re-layouts: 3.9 us -> none  [the longest x1 1.95 us: per_device(): natural = jnp.take(block_order, row_ids // block_rows)]
  transfers between devices with their start and end apart: 4 -> 0, of which waited for: 3 -> 0; matrix products, arithmetic and copies ran while one was open for 17% -> 0% of each run, Pallas kernels for 0% -> 0%
where the time goes in v1:
time: 91.4 us; the launch traced here: 91 us
  Pallas kernels  76.9 us (84%)
  local copies, waits for them, and re-layouts  7.91 us (9%)
  between operations  4.59 us (5%)
  other arithmetic  1.62 us (2%)
    pallas_call x1, Pallas kernels, column_plan(): pl.pallas_call(functools.partial(attend_kernel, sizes), out_shape=(jax.Sh...  76.9 us
    unnamed x19, local copies, waits for them, and re-layouts  7.25 us

profile of v1, /device:TPU:0, one launch (start us, length us, event | category | flops | bytes accessed | tf_op | source)
XLA Modules:
  0.0 91.0 jit_solution(6511427205115613694)
XLA Ops:
  0.6 0.0 copy-start.8
  0.6 0.6 copy-done.8
  1.3 0.1 dynamic_slice.3
  1.4 0.0 copy-start.5
  1.4 0.1 maximum_bitcast_fusion.freq_ref
  1.5 0.6 fusion.3
  5.9 0.0 copy-start.6
  5.9 0.0 copy-start.7
  6.0 0.0 copy-done.5
  6.0 0.6 copy-done.6
  6.6 0.0 copy-done.7
  6.6 0.0 copy-start
  6.6 1.2 %copy-done = bf16[128,4096]{1,0:T(8,128)(2,1)S(1)} copy-done((bf16[128,4096]{1,0:T(8,128)(2,1)S(1)}, bf16[128,4096]{1,0:T(8,128)(2,1)}, u32[]{:S(2)}) %copy-start) | copy-done | bytes 1048600
  7.8 0.0 copy-start.1
  7.8 1.2 %copy-done.1 = bf16[512,1024]{1,0:T(8,128)(2,1)S(1)} copy-done((bf16[512,1024]{1,0:T(8,128)(2,1)S(1)}, bf16[512,1024]{1,0:T(8,128)(2,1)}, u32[]{:S(2)}) %copy-start.1) | copy-done | bytes 1048600
  9.1 0.0 copy-start.2
  9.1 0.9 copy-done.2
  10.0 0.0 copy-start.3
  10.0 0.9 %copy-done.3 = bf16[512,256]{1,0:T(8,128)(2,1)S(1)} copy-done((bf16[512,256]{1,0:T(8,128)(2,1)S(1)}, bf16[512,256]{1,0:T(8,128)(2,1)}, u32[]{:S(2)}) %copy-start.3) | copy-done | bytes 262168
  10.9 0.0 copy-start.4
  10.9 0.9 %copy-done.4 = bf16[512,256]{1,0:T(8,128)(2,1)S(1)} copy-done((bf16[512,256]{1,0:T(8,128)(2,1)S(1)}, bf16[512,256]{1,0:T(8,128)(2,1)}, u32[]{:S(2)}) %copy-start.4) | copy-done | bytes 262168
  11.9 76.9 %shard_map.104 = (bf16[128,1024]{1,0:T(8,128)(2,1)S(1)}, bf16[64,2,4,128]{3,2,1,0:T(4,128)(2,1)S(1)}) custom-call(s32[16]{0:T(128)S(1)} %copy-done.6, s32[16]{0:T(128)S(1)} %copy-done.7, f32[1,128]{1,0:T(1,128)S(1)} %maximum_bitcast_fusion.freq_ref, f32[1,4096]{1,0:T(1,128)S(1)} %bitcast.15, bf16[128,4096]{1,0:T(8,128)(2,1)S(1)} %copy-done, ...), custom_call_target="tpu_custom_call" | custom-call | tf_op jit(solution)/shard_map/pallas_call | solution.py:579
  88.8 0.5 broadcast_select_fusion.5
  89.4 1.0 %pad_maximum_fusion.1 = bf16[128,2,2,128]{3,2,1,0:T(2,128)(2,1)} fusion(bf16[128,2,1,128]{3,2,1,0:T(2,128)(2,1)S(1)} %get-tuple-element.7, bf16[128,2,1,128]{3,2,1,0:T(2,128)(2,1)S(1)} %get-tuple-element.6), kind=kLoop, calls=%fused_computation.16 | loop fusion | flops 262144 | bytes 262144 | tf_op jit(solution)/shard_map/stack | solution.py:639
  90.3 0.7 copy.12
  (2 shorter events, 0.0 us)
Async XLA Ops:
  0.6 0.7 copy-start.8
  1.4 4.6 %copy-start.5 = (f32[4096]{0:T(1024)S(1)}, f32[4096]{0:T(1024)}, u32[]{:S(2)}) copy-start(f32[4096]{0:T(1024)} %param.10) | copy-start | bytes 49156
  5.9 0.7 copy-start.6
  5.9 0.7 copy-start.7
  6.6 1.2 %copy-start = (bf16[128,4096]{1,0:T(8,128)(2,1)S(1)}, bf16[128,4096]{1,0:T(8,128)(2,1)}, u32[]{:S(2)}) copy-start(bf16[128,4096]{1,0:T(8,128)(2,1)} %tok_in.1) | copy-start | bytes 3145732
  7.8 1.2 %copy-start.1 = (bf16[512,1024]{1,0:T(8,128)(2,1)S(1)}, bf16[512,1024]{1,0:T(8,128)(2,1)}, u32[]{:S(2)}) copy-start(bf16[512,1024]{1,0:T(8,128)(2,1)} %wq_in.1) | copy-start | bytes 3145732
  9.1 0.9 copy-start.2
  10.0 0.9 %copy-start.3 = (bf16[512,256]{1,0:T(8,128)(2,1)S(1)}, bf16[512,256]{1,0:T(8,128)(2,1)}, u32[]{:S(2)}) copy-start(bf16[512,256]{1,0:T(8,128)(2,1)} %wk_in.1) | copy-start | bytes 786436
  10.9 0.9 %copy-start.4 = (bf16[512,256]{1,0:T(8,128)(2,1)S(1)}, bf16[512,256]{1,0:T(8,128)(2,1)}, u32[]{:S(2)}) copy-start(bf16[512,256]{1,0:T(8,128)(2,1)} %wv_in.1) | copy-start | bytes 786436

commit v2 on v1

--- a/solution.py
+++ b/solution.py
@@ -348,8 +348,7 @@
             tok.at[c, my_half], tok.at[c, my_half], sib_send.at[c], sib_recv.at[c], sibling
         )
 
-    for s in range(1, A):
-
+    def token_step(s):
         @pl.when(a >= s)
         def _():
             c = a - s
@@ -372,7 +371,64 @@
 
             share(c).start()
 
-    own_tok.wait()
+    def pick(s):
+        value, bit = 0, 1
+        while bit < A:
+            value = value + bit * ((a // bit + s // bit) % 2)
+            bit *= 2
+        return value
+
+    def kv_peer(dy, da):
+        return dev(x, a - unit + (unit + da) % 2, (y + dy) % Y)
+
+    kv_plan = [(dy, da) for dy in range(Y) for da in range(2) if (dy, da) != (0, 0)]
+
+    def kv_push(s, c, index, dy, da):
+        src = kvbuf.at[unit, c * Y + y]
+        return remote(src, src, kv_send.at[s, index], kv_recv.at[unit, c, y], kv_peer(dy, da))
+
+    def normalize(s):
+        c = pick(s)
+        if s == 0:
+            own_tok.wait()
+        else:
+            other = tok.at[c, other_half]
+            remote(other, other, sib_send.at[c], sib_recv.at[c], sibling).wait_recv()
+
+        def block(i, carry):
+            span = pl.ds(pl.multiple_of(i * 16, 16), 16)
+            inputs = tok[c, span].astype(jnp.float32)
+            mean = jnp.mean(inputs * inputs, -1, keepdims=True)
+            normed[c, span] = (inputs * lax.rsqrt(mean + 1e-05) * gain_ref[...]).astype(
+                jnp.bfloat16
+            )
+            return carry
+
+        lax.fori_loop(0, rows // 16, block, 0, unroll=2)
+
+    def project(s, carry):
+        c = pick(s)
+        cosine = csbuf[0, c]
+        sine = csbuf[1, c]
+
+        def turn(v):
+            return v * cosine + pltpu.roll(v, HD // 2, 1) * sine
+
+        raw = jnp.dot(normed[c], wbuf[:, QW:], preferred_element_type=jnp.float32)
+        kvbuf[unit, c * Y + y] = jnp.where(unit == 0, turn(raw), raw).astype(jnp.bfloat16)
+        product = jnp.dot(normed[c], wbuf[:, :QW], preferred_element_type=jnp.float32)
+        for index, (dy, da) in enumerate(kv_plan):
+            kv_push(s, c, index, dy, da).start()
+        for h in range(hpg):
+            qbuf[c, :, h * HD : (h + 1) * HD] = turn(product[:, h * HD : (h + 1) * HD]).astype(
+                jnp.bfloat16
+            )
+        return carry
+
+    normalize(0)
+    for s in range(1, A - 1):
+        token_step(s)
+        normalize(s)
     for o in range(A):
         t = (a + o) % A
         for i, j in plane:
@@ -386,56 +442,10 @@
                     sibling,
                 ).wait_recv()
 
-    def pick(s):
-        value, bit = 0, 1
-        while bit < A:
-            value = value + bit * ((a // bit + s // bit) % 2)
-            bit *= 2
-        return value
-
-    def kv_peer(dy, da):
-        return dev(x, a - unit + (unit + da) % 2, (y + dy) % Y)
-
-    kv_plan = [(dy, da) for dy in range(Y) for da in range(2) if (dy, da) != (0, 0)]
-
-    def kv_push(s, c, index, dy, da):
-        src = kvbuf.at[unit, c * Y + y]
-        return remote(src, src, kv_send.at[s, index], kv_recv.at[unit, c, y], kv_peer(dy, da))
-
-    def project(s, carry):
-        c = pick(s)
-
-        @pl.when(s > 0)
-        def _():
-            remote(
-                tok.at[c, other_half],
-                tok.at[c, other_half],
-                sib_send.at[c],
-                sib_recv.at[c],
-                sibling,
-            ).wait_recv()
-
-        inputs = tok[c].astype(jnp.float32)
-        mean = jnp.mean(inputs * inputs, -1, keepdims=True)
-        normed[...] = (inputs * lax.rsqrt(mean + 1e-05) * gain_ref[...]).astype(jnp.bfloat16)
-        cosine = csbuf[0, c]
-        sine = csbuf[1, c]
-        product = jnp.dot(normed[...], wbuf[...], preferred_element_type=jnp.float32)
-
-        def turn(v):
-            return v * cosine + pltpu.roll(v, HD // 2, 1) * sine
-
-        raw = product[:, QW:]
-        kvbuf[unit, c * Y + y] = jnp.where(unit == 0, turn(raw), raw).astype(jnp.bfloat16)
-        for h in range(hpg):
-            qbuf[c, :, h * HD : (h + 1) * HD] = turn(product[:, h * HD : (h + 1) * HD]).astype(
-                jnp.bfloat16
-            )
-        for index, (dy, da) in enumerate(kv_plan):
-            kv_push(s, c, index, dy, da).start()
-        return carry
-
-    lax.fori_loop(0, A, project, 0)
+    lax.fori_loop(0, A - 1, project, 0)
+    token_step(A - 1)
+    normalize(A - 1)
+    project(A - 1, 0)
 
     for s in range(A):
         c = pick(s)
@@ -587,7 +597,7 @@
         scratch_shapes=[
             pltpu.VMEM((A, rows, width), jnp.bfloat16),
             pltpu.VMEM((width, QW + HD), jnp.bfloat16),
-            pltpu.VMEM((rows, width), jnp.bfloat16),
+            pltpu.VMEM((A, rows, width), jnp.bfloat16),
             pltpu.VMEM((A, rows, QW), jnp.bfloat16),
             pltpu.VMEM((2, n_seq, rows, HD), jnp.bfloat16),
             pltpu.VMEM((2, A, rows, HD), jnp.float32),
@@ -610,7 +620,7 @@
             dma((A,)),
         ],
         compiler_params=pltpu.CompilerParams(
-            collective_id=0, has_side_effects=True, vmem_limit_bytes=48 * 1024 * 1024
+            collective_id=0, has_side_effects=True
         ),
     )(
         block_order,

time: 91.4 us -> 87.2 us (0.954)
  local copies, waits for them, and re-layouts: 7.91 us -> 2.1 us
  other arithmetic: 1.62 us -> 3.04 us
    unnamed x19 -> x7, local copies, waits for them, and re-layouts: 7.25 us -> 1.36 us
where the time goes in v2:
time: 87.2 us; the launch traced here: 87 us
  Pallas kernels  77.1 us (88%)
  between operations  4.71 us (5%)
  other arithmetic  3.04 us (3%)
  local copies, waits for them, and re-layouts  2.1 us (2%)
    pallas_call x1, Pallas kernels, column_plan(): pl.pallas_call(functools.partial(attend_kernel, sizes), out_shape=(jax.Sh...  77.1 us

profile of v2, /device:TPU:0, one launch (start us, length us, event | category | flops | bytes accessed | tf_op | source)
XLA Modules:
  0.0 87.0 jit_solution(7592777133551645773)
XLA Ops:
  0.6 0.0 copy-start.2
  0.6 0.6 copy-done.2
  1.3 0.1 dynamic_slice.3
  1.4 0.6 maximum_bitcast_fusion.freq_ref
  2.0 0.7 fusion.3
  6.7 0.0 copy-start
  6.7 77.1 %shard_map.104 = (bf16[128,1024]{1,0:T(8,128)(2,1)}, bf16[64,2,4,128]{3,2,1,0:T(4,128)(2,1)}) custom-call(s32[16]{0:T(128)} %order_ref.1, s32[16]{0:T(128)} %docs_ref.1, f32[1,128]{1,0:T(1,128)} %maximum_bitcast_fusion.freq_ref, f32[1,4096]{1,0:T(1,128)} %bitcast.17, bf16[128,4096]{1,0:T(8,128)(2,1)} %tok_in.1, bf16[512,1024]{1,0:T(8,128)(2,1)} %wq_in.1, ...), custom_call_target="tpu_custom_call" | custom-call | tf_op jit(solution)/shard_map/pallas_call | solution.py:589
  83.8 0.0 copy-done
  83.8 0.9 %broadcast_select_fusion.7 = (bf16[64,1,8,128]{3,2,1,0:T(8,128)(2,1)S(1)}, bf16[64,1,8,128]{3,2,1,0:T(8,128)(2,1)S(1)}) fusion(bf16[64,1,8,128]{3,2,1,0:T(8,128)(2,1)S(1)} %bitcast.13, bf16[64,1,8,128]{3,2,1,0:T(8,128)(2,1)} %bitcast.16, pred[]{:T(512)S(6)} %eq.42), kind=kLoop, calls=%fused_computation.18 | loop fusion | flops 131072 | bytes 524289 | tf_op jit(solution)/shard_map/jit(_where)/select_n | solution.py:641
  84.7 0.5 broadcast_select_fusion.5
  85.3 0.0 copy-start.1
  85.3 1.0 %pad_maximum_fusion.1 = bf16[128,2,2,128]{3,2,1,0:T(2,128)(2,1)} fusion(bf16[128,2,1,128]{3,2,1,0:T(2,128)(2,1)S(1)} %get-tuple-element.7, bf16[128,2,1,128]{3,2,1,0:T(2,128)(2,1)S(1)} %get-tuple-element.6), kind=kLoop, calls=%fused_computation.16 | loop fusion | flops 262144 | bytes 262144 | tf_op jit(solution)/shard_map/stack | solution.py:649
  86.3 0.0 copy-done.1
  86.3 0.7 copy.12
  (1 shorter events, 0.0 us)
Async XLA Ops:
  0.6 0.7 copy-start.2
  6.7 77.1 %copy-start = (bf16[64,2,4,128]{3,2,1,0:T(4,128)(2,1)S(1)}, bf16[64,2,4,128]{3,2,1,0:T(4,128)(2,1)}, u32[]{:S(2)}) copy-start(bf16[64,2,4,128]{3,2,1,0:T(4,128)(2,1)} %prev_in.1) | copy-start | bytes 393220
  85.3 1.0 %copy-start.1 = (bf16[128,1024]{1,0:T(8,128)(2,1)S(1)}, bf16[128,1024]{1,0:T(8,128)(2,1)}, u32[]{:S(2)}) copy-start(bf16[128,1024]{1,0:T(8,128)(2,1)} %get-tuple-element.16) | copy-start | bytes 786436

commit v3 on v2

--- a/solution.py
+++ b/solution.py
@@ -305,15 +305,6 @@
     def row_positions(c):
         return row_values(c, lambda n: n) * blk + row_id % blk
 
-    def angles(c, carry):
-        angle = row_positions(c).astype(jnp.float32) * freq_ref[...]
-        csbuf[0, c] = jnp.cos(angle)
-        sine = jnp.sin(angle)
-        csbuf[1, c] = jnp.where(lane < HD // 2, -sine, sine)
-        return carry
-
-    lax.fori_loop(0, A, angles, 0)
-
     for o in range(1, A):
         t = (a + o) % A
         src = wbuf.at[w_rows(t, y, x)]
@@ -424,6 +415,30 @@
                 jnp.bfloat16
             )
         return carry
+
+    step_angle = (row_id % blk).astype(jnp.float32) * freq_ref[...]
+    step_cos = jnp.cos(step_angle)
+    step_sin = jnp.sin(step_angle)
+    sign = jnp.where(lane < HD // 2, -1.0, 1.0)
+    entry_id = lax.broadcasted_iota(jnp.int32, (A * slots, 1), 0)
+    entries = jnp.zeros((A * slots, 1), jnp.int32)
+    for c in range(A):
+        for i in range(slots):
+            entries = jnp.where(
+                entry_id == c * slots + i, order_ref[(c * Y + y) * slots + i], entries
+            )
+    base_angle = (entries * blk).astype(jnp.float32) * freq_ref[...]
+    base_cos = jnp.cos(base_angle)
+    base_sin = jnp.sin(base_angle)
+    for c in range(A):
+        row_cos = jnp.broadcast_to(base_cos[c * slots : c * slots + 1], (rows, HD))
+        row_sin = jnp.broadcast_to(base_sin[c * slots : c * slots + 1], (rows, HD))
+        for i in range(1, slots):
+            k = c * slots + i
+            row_cos = jnp.where(row_id // blk == i, base_cos[k : k + 1], row_cos)
+            row_sin = jnp.where(row_id // blk == i, base_sin[k : k + 1], row_sin)
+        csbuf[0, c] = row_cos * step_cos - row_sin * step_sin
+        csbuf[1, c] = (row_sin * step_cos + row_cos * step_sin) * sign
 
     normalize(0)
     for s in range(1, A - 1):

time: 87.2 us -> 87.2 us (level)
  no operation moved by 1% of the time
where the time goes in v3:
time: 87.2 us; the launch traced here: 87 us
  Pallas kernels  77.1 us (88%)
  between operations  4.71 us (5%)
  other arithmetic  3.04 us (3%)
  local copies, waits for them, and re-layouts  2.1 us (2%)
    pallas_call x1, Pallas kernels, column_plan(): pl.pallas_call(functools.partial(attend_kernel, sizes), out_shape=(jax.Sh...  77.1 us

profile of v3, /device:TPU:0, one launch (start us, length us, event | category | flops | bytes accessed | tf_op | source)
XLA Modules:
  0.0 87.0 jit_solution(1806614724321296268)
XLA Ops:
  0.6 0.0 copy-start.2
  0.6 0.6 copy-done.2
  1.3 0.1 dynamic_slice.3
  1.4 0.6 maximum_bitcast_fusion.freq_ref
  2.0 0.7 fusion.3
  6.7 0.0 copy-start
  6.7 77.1 %shard_map.104 = (bf16[128,1024]{1,0:T(8,128)(2,1)}, bf16[64,2,4,128]{3,2,1,0:T(4,128)(2,1)}) custom-call(s32[16]{0:T(128)} %order_ref.1, s32[16]{0:T(128)} %docs_ref.1, f32[1,128]{1,0:T(1,128)} %maximum_bitcast_fusion.freq_ref, f32[1,4096]{1,0:T(1,128)} %bitcast.17, bf16[128,4096]{1,0:T(8,128)(2,1)} %tok_in.1, bf16[512,1024]{1,0:T(8,128)(2,1)} %wq_in.1, ...), custom_call_target="tpu_custom_call" | custom-call | tf_op jit(solution)/shard_map/pallas_call | solution.py:604
  83.8 0.0 copy-done
  83.8 0.9 %broadcast_select_fusion.7 = (bf16[64,1,8,128]{3,2,1,0:T(8,128)(2,1)S(1)}, bf16[64,1,8,128]{3,2,1,0:T(8,128)(2,1)S(1)}) fusion(bf16[64,1,8,128]{3,2,1,0:T(8,128)(2,1)S(1)} %bitcast.13, bf16[64,1,8,128]{3,2,1,0:T(8,128)(2,1)} %bitcast.16, pred[]{:T(512)S(6)} %eq.42), kind=kLoop, calls=%fused_computation.18 | loop fusion | flops 131072 | bytes 524289 | tf_op jit(solution)/shard_map/jit(_where)/select_n | solution.py:656
  84.7 0.5 broadcast_select_fusion.5
  85.3 0.0 copy-start.1
  85.3 1.0 %pad_maximum_fusion.1 = bf16[128,2,2,128]{3,2,1,0:T(2,128)(2,1)} fusion(bf16[128,2,1,128]{3,2,1,0:T(2,128)(2,1)S(1)} %get-tuple-element.7, bf16[128,2,1,128]{3,2,1,0:T(2,128)(2,1)S(1)} %get-tuple-element.6), kind=kLoop, calls=%fused_computation.16 | loop fusion | flops 262144 | bytes 262144 | tf_op jit(solution)/shard_map/stack | solution.py:664
  86.2 0.0 copy-done.1
  86.2 0.7 copy.12
  (1 shorter events, 0.0 us)
Async XLA Ops:
  0.6 0.7 copy-start.2
  6.7 77.1 %copy-start = (bf16[64,2,4,128]{3,2,1,0:T(4,128)(2,1)S(1)}, bf16[64,2,4,128]{3,2,1,0:T(4,128)(2,1)}, u32[]{:S(2)}) copy-start(bf16[64,2,4,128]{3,2,1,0:T(4,128)(2,1)} %prev_in.1) | copy-start | bytes 393220
  85.3 1.0 %copy-start.1 = (bf16[128,1024]{1,0:T(8,128)(2,1)S(1)}, bf16[128,1024]{1,0:T(8,128)(2,1)}, u32[]{:S(2)}) copy-start(bf16[128,1024]{1,0:T(8,128)(2,1)} %get-tuple-element.16) | copy-start | bytes 786436
